TPU v7x, 256 devices: a whole 4x4x8 slice. The times are simulated.
256 devices in a mesh: gz: 8 (over z), gx: 4 (over x), gy: 8 (over y, core).
Axes of the slice: x: 4, y: 4, z: 8, core: 2. Of those that a mesh axis runs over, the one named last changes fastest.
Arguments:
- density: float32 [256, 1024, 1024], P('gz', 'gy', 'gx'), may hold values from 0 to 1
- mask: int32 [32, 128, 128], P('gz', 'gy', 'gx'), may hold values from 0 to 3
Outputs:
- filtered: float32 [256, 1024, 1024], P(('gz', 'gx'), 'gy')
- projected: float32 [256, 1024, 1024], P(('gz', 'gx'), 'gy')
Inputs may be any that keep to these rules, and one draw needn't show every extreme that they name: `mask`: code 0 marks a void block, 1 a solid block, 2 and 3 design blocks.
All inputs are finite; a program needn't handle non-finite values.
Results may differ from a plain program's by a relative error of at most 0.0003.
Values sent between devices are 32-bit elements; how exact they have to be, the bound alone decides.
A program may use at most 128 MiB of HBM per device.

v0:
```python
import functools
import math

import jax
import jax.numpy as jnp
from jax import lax
from jax.experimental import pallas as pl
from jax.experimental.pallas import tpu as pltpu
from jax.sharding import PartitionSpec as P

RADIUS = 6
CELLS = 8
LANES = 128
SUBLANES = 8

sharpness = 8.0
threshold = 0.5
MESH = pl.DeviceIdType.MESH


def hat(rows, cols, offset):
    row = lax.broadcasted_iota(jnp.int32, (rows, cols), 0)
    col = lax.broadcasted_iota(jnp.int32, (rows, cols), 1)
    return jnp.maximum(RADIUS + 1 - jnp.abs(col + offset - row), 0).astype(jnp.float32)


def halves(values):
    high = values.astype(jnp.bfloat16)
    low = (values - high.astype(jnp.float32)).astype(jnp.bfloat16)
    return high, low


def projection(filtered):
    top = math.tanh(sharpness * threshold)
    bottom = top + math.tanh(sharpness * (1.0 - threshold))
    return (top + jnp.tanh(sharpness * (filtered - threshold))) * (1.0 / bottom)


def one_side(reach):
    return reach * (RADIUS + 1) - reach * (reach + 1) // 2


def dot(a, b):
    return jnp.dot(a, b, preferred_element_type=jnp.float32)


def x_filter(chunks, w_own, w_edge, xs, first):
    size, columns = chunks[0].shape
    high, low = zip(*[halves(chunk) for chunk in chunks])
    none = jnp.zeros((size, LANES), jnp.bfloat16)
    for c in range(len(chunks)):
        total = dot(high[c], w_own[...]) + dot(low[c], w_own[...])
        for part in (high, low):
            left = part[c - 1][:, columns - LANES :] if c > 0 else none
            right = part[c + 1][:, :LANES] if c < len(chunks) - 1 else none
            total = total + dot(jnp.concatenate([left, right], 1), w_edge[...])
        at = pl.ds(c * columns, columns)
        xs[pl.ds(first, size), at], xs[pl.ds(first + size, size), at] = halves(total)


def y_filter(xs, scale, scale_z, columns, put):
    rows, width = scale.shape
    own = hat(rows, rows, 0).astype(jnp.bfloat16)
    edge = jnp.concatenate([hat(rows, SUBLANES, -SUBLANES), hat(rows, SUBLANES, rows)], 1)
    edge = edge.astype(jnp.bfloat16)
    own = jnp.concatenate([own, own], 1)
    edge = jnp.concatenate([edge, edge], 1)
    for c in range(width // columns):
        at = pl.ds(c * columns, columns)
        summed = dot(own, xs[pl.ds(0, 2 * rows), at])
        summed = summed + dot(edge, xs[pl.ds(2 * rows, 4 * SUBLANES), at])
        put(at, summed * (scale[:, at] * scale_z))


def inverse_count(position, length):
    left = one_side(jnp.minimum(position, RADIUS))
    right = one_side(jnp.minimum(length - 1 - position, RADIUS))
    return 1.0 / (RADIUS + 1 + left + right).astype(jnp.float32)


def layer_of(k, layers):
    return jnp.where(lax.axis_index("gx") == 0, layers - 1 - k, k)


def scale_along_z(sizes, k, layers, columns):
    nz, nx, ny = sizes
    level = (lax.axis_index("gz") * nx + lax.axis_index("gx")) * layers + layer_of(k, layers)
    level = jnp.full((SUBLANES, columns), level, jnp.int32)
    return inverse_count(level, nz * nx * layers)[0:1]


def kernel(
    sizes,
    density,
    mask,
    fstage,
    pstage,
    lrecv,
    lyb,
    scale,
    w_own,
    w_edge,
    phys,
    codes,
    masks,
    zf,
    recv,
    yb,
    xs,
    load_sem,
    mask_sem,
    hmask_send,
    hmask_recv,
    halo_send,
    halo_recv,
    send_sem,
    recv_sem,
    y_send,
    y_recv,
    e_send,
    e_recv,
):
    nz, nx, ny = sizes
    planes, rows, columns = density.shape
    blocks = mask.shape[0]
    layers = planes // nx
    gz, gx, gy = lax.axis_index("gz"), lax.axis_index("gx"), lax.axis_index("gy")
    has_up, has_down = gz > 0, gz < nz - 1
    has_prev, has_next = gy > 0, gy < ny - 1

    def load(b):
        part = pl.ds(b * CELLS, CELLS)
        return pltpu.make_async_copy(
            density.at[part], phys.at[pl.ds(RADIUS + b * CELLS, CELLS)], load_sem.at[b]
        )

    mask_copy = pltpu.make_async_copy(mask, masks.at[pl.ds(1, blocks)], mask_sem)
    mask_copy.start()
    for b in range(blocks):
        load(b).start()

    barrier = pltpu.get_barrier_semaphore()

    def greet(**where):
        pl.semaphore_signal(barrier, inc=1, device_id=where, device_id_type=MESH)

    pl.when(has_up)(lambda: greet(gz=gz - 1))
    pl.when(has_down)(lambda: greet(gz=gz + 1))
    pl.when(has_prev)(lambda: greet(gy=gy - 1))
    pl.when(has_next)(lambda: greet(gy=gy + 1))
    for step in range(1, nx):
        greet(gx=lax.rem(gx + step, nx))

    def to_next(j):
        return pltpu.make_async_remote_copy(
            src_ref=density.at[planes - 1 - j],
            dst_ref=phys.at[RADIUS - 1 - j],
            send_sem=halo_send.at[0, j],
            recv_sem=halo_recv.at[0, j],
            device_id={"gz": gz + 1},
            device_id_type=MESH,
        )

    def to_previous(j):
        return pltpu.make_async_remote_copy(
            src_ref=density.at[j],
            dst_ref=phys.at[RADIUS + planes + j],
            send_sem=halo_send.at[1, j],
            recv_sem=halo_recv.at[1, j],
            device_id={"gz": gz - 1},
            device_id_type=MESH,
        )

    def mask_next():
        return pltpu.make_async_remote_copy(
            src_ref=mask.at[blocks - 1],
            dst_ref=masks.at[0],
            send_sem=hmask_send.at[0],
            recv_sem=hmask_recv.at[0],
            device_id={"gz": gz + 1},
            device_id_type=MESH,
        )

    def mask_previous():
        return pltpu.make_async_remote_copy(
            src_ref=mask.at[0],
            dst_ref=masks.at[blocks + 1],
            send_sem=hmask_send.at[1],
            recv_sem=hmask_recv.at[1],
            device_id={"gz": gz - 1},
            device_id_type=MESH,
        )

    def spread(b):
        small = masks[b].astype(jnp.float32).astype(jnp.bfloat16)
        mrows, mcols = small.shape
        r = lax.broadcasted_iota(jnp.int32, (rows, mrows), 0) // CELLS
        m = lax.broadcasted_iota(jnp.int32, (rows, mrows), 1)
        tall = dot(jnp.where(r == m, 1.0, 0.0).astype(jnp.bfloat16), small)
        c = lax.broadcasted_iota(jnp.int32, (mcols, columns), 1) // CELLS
        n = lax.broadcasted_iota(jnp.int32, (mcols, columns), 0)
        wide = jnp.where(c == n, 1.0, 0.0).astype(jnp.bfloat16)
        codes[b] = dot(tall.astype(jnp.bfloat16), wide)

    def apply_mask(row, b):
        code = codes[b]
        phys[row] = jnp.where(code < 0.5, 0.0, jnp.where(code < 1.5, 1.0, phys[row]))

    def piece(k, p, row):
        return pltpu.make_async_remote_copy(
            src_ref=zf.at[row],
            dst_ref=recv.at[k, gx],
            send_sem=send_sem.at[k, p],
            recv_sem=recv_sem.at[k, gx],
            device_id={"gx": p},
            device_id_type=MESH,
        )

    edges = (pl.ds(0, SUBLANES), pl.ds(rows - SUBLANES, SUBLANES))
    inside = pl.ds(SUBLANES, rows - 2 * SUBLANES)

    def edge_piece(side, p, row):
        return pltpu.make_async_remote_copy(
            src_ref=zf.at[row, edges[side]],
            dst_ref=lrecv.at[gx, edges[side]],
            send_sem=e_send.at[side, p],
            recv_sem=e_recv.at[side, gx],
            device_id={"gx": p},
            device_id_type=MESH,
        )

    def inner_piece(p, row):
        return pltpu.make_async_remote_copy(
            src_ref=zf.at[row, inside],
            dst_ref=lrecv.at[gx, inside],
            send_sem=send_sem.at[layers - 1, p],
            recv_sem=recv_sem.at[layers - 1, gx],
            device_id={"gx": p},
            device_id_type=MESH,
        )

    def row_of(k, p):
        return layers - 1 - k if p == 0 else p * layers + k

    def z_filter(row):
        part = rows // 4
        for i in range(4):
            at = pl.ds(i * part, part)
            run = phys[row + RADIUS, at]
            total = run
            for d in range(1, RADIUS + 1):
                run = run + (phys[row + RADIUS - d, at] + phys[row + RADIUS + d, at])
                total = total + run
            zf[row, at] = total

    def z_send(k, p):
        row = row_of(k, p)
        z_filter(row)

        @pl.when(gx != p)
        def _():
            piece(k, p, row).start()

        @pl.when(gx == p)
        def _():
            pltpu.make_async_copy(zf.at[row], recv.at[k, gx], recv_sem.at[k, gx]).start()

    def z_step(k, carry):
        for p in range(nx):
            z_send(k, p)
        return carry

    def mask_block(b):
        spread(b + 1)
        load(b).wait()

        def one(i, carry):
            apply_mask(RADIUS + b * CELLS + i, b + 1)
            return carry

        lax.fori_loop(0, CELLS, one, 0)

    mask_copy.wait()
    ready = 0
    for p in range(nx):
        need = min(blocks, (row_of(0, p) + RADIUS) // CELLS + 1)
        for b in range(ready, need):
            mask_block(b)
        if p == 0:
            count = nx - 1
            for there in (has_up, has_down, has_prev, has_next):
                count = count + there.astype(jnp.int32)
            pl.semaphore_wait(barrier, count)
        ready = max(ready, need)
        z_send(0, p)
    for b in range(ready, blocks):
        mask_block(b)

    @pl.when(has_down)
    def _():
        mask_next().start()
        for j in range(RADIUS):
            to_next(j).start()

    @pl.when(has_up)
    def _():
        mask_previous().start()
        for j in range(RADIUS):
            to_previous(j).start()

    @pl.when(jnp.logical_not(has_up))
    def _():
        phys[pl.ds(0, RADIUS)] = jnp.zeros((RADIUS, rows, columns), jnp.float32)

    @pl.when(jnp.logical_not(has_down))
    def _():
        phys[pl.ds(RADIUS + planes, RADIUS)] = jnp.zeros((RADIUS, rows, columns), jnp.float32)

    @pl.when(jnp.logical_not(has_prev))
    def _():
        lyb[:, pl.ds(0, SUBLANES)] = jnp.zeros((nx, SUBLANES, columns), jnp.float32)
        yb[:, :, pl.ds(0, SUBLANES)] = jnp.zeros((layers - 1, nx, SUBLANES, columns), jnp.float32)

    @pl.when(jnp.logical_not(has_next))
    def _():
        lyb[:, pl.ds(SUBLANES, SUBLANES)] = jnp.zeros((nx, SUBLANES, columns), jnp.float32)
        yb[:, :, pl.ds(SUBLANES, SUBLANES)] = jnp.zeros((layers - 1, nx, SUBLANES, columns), jnp.float32)

    free = layers - RADIUS
    lax.fori_loop(1, free, z_step, 0)

    w_own[...] = hat(columns, columns, 0).astype(jnp.bfloat16)
    w_edge[pl.ds(0, LANES)] = hat(LANES, columns, LANES).astype(jnp.bfloat16)
    w_edge[pl.ds(LANES, LANES)] = hat(LANES, columns, -columns).astype(jnp.bfloat16)

    width = nx * columns
    scale_y = inverse_count(
        gy * rows + lax.broadcasted_iota(jnp.int32, (rows, LANES), 0), rows * ny
    )
    for c in range(0, width, LANES):
        lane = c + lax.broadcasted_iota(jnp.int32, (SUBLANES, LANES), 1)
        scale_x = inverse_count(lane, width)
        scale[:, pl.ds(c, LANES)] = scale_y * scale_x[0:1]

    @pl.when(has_up)
    def _():
        mask_previous().wait_send()
        pltpu.make_async_copy(mask.at[0], masks.at[0], hmask_recv.at[0]).wait()
        spread(0)

    @pl.when(has_down)
    def _():
        mask_next().wait_send()
        pltpu.make_async_copy(mask.at[0], masks.at[blocks + 1], hmask_recv.at[1]).wait()
        spread(blocks + 1)

    def take_halo(k):
        j = k - free

        @pl.when(has_up)
        def _():
            row = RADIUS - 1 - j
            pltpu.make_async_copy(density.at[0], phys.at[row], halo_recv.at[0, j]).wait()
            apply_mask(row, 0)

        @pl.when(has_down)
        def _():
            row = RADIUS + planes + j
            pltpu.make_async_copy(density.at[0], phys.at[row], halo_recv.at[1, j]).wait()
            apply_mask(row, blocks + 1)

    def halo_step(k, carry):
        take_halo(k)
        return z_step(k, carry)

    final = layers - 1
    lax.fori_loop(free, final, halo_step, 0)

    take_halo(final)
    for p in range(nx):
        row = row_of(final, p)
        z_filter(row)

        @pl.when(gx != p)
        def _():
            edge_piece(0, p, row).start()
            edge_piece(1, p, row).start()

        @pl.when(gx == p)
        def _():
            for side in range(2):
                pltpu.make_async_copy(
                    zf.at[row, edges[side]], lrecv.at[gx, edges[side]], e_recv.at[side, gx]
                ).start()
            pltpu.make_async_copy(
                zf.at[row, inside], lrecv.at[gx, inside], recv_sem.at[final, gx]
            ).start()

    for p in range(nx):

        @pl.when(gx != p)
        def _():
            inner_piece(p, row_of(final, p)).start()

    def y_previous(k):
        return pltpu.make_async_remote_copy(
            src_ref=recv.at[k, :, pl.ds(0, SUBLANES)],
            dst_ref=yb.at[k, :, pl.ds(SUBLANES, SUBLANES)],
            send_sem=y_send.at[k, 0],
            recv_sem=y_recv.at[k, 1],
            device_id={"gy": gy - 1},
            device_id_type=MESH,
        )

    def y_next(k):
        return pltpu.make_async_remote_copy(
            src_ref=recv.at[k, :, pl.ds(rows - SUBLANES, SUBLANES)],
            dst_ref=yb.at[k, :, pl.ds(0, SUBLANES)],
            send_sem=y_send.at[k, 1],
            recv_sem=y_recv.at[k, 0],
            device_id={"gy": gy + 1},
            device_id_type=MESH,
        )

    def last_previous():
        return pltpu.make_async_remote_copy(
            src_ref=lrecv.at[:, pl.ds(0, SUBLANES)],
            dst_ref=lyb.at[:, pl.ds(SUBLANES, SUBLANES)],
            send_sem=y_send.at[final, 0],
            recv_sem=y_recv.at[final, 1],
            device_id={"gy": gy - 1},
            device_id_type=MESH,
        )

    def last_next():
        return pltpu.make_async_remote_copy(
            src_ref=lrecv.at[:, pl.ds(rows - SUBLANES, SUBLANES)],
            dst_ref=lyb.at[:, pl.ds(0, SUBLANES)],
            send_sem=y_send.at[final, 1],
            recv_sem=y_recv.at[final, 0],
            device_id={"gy": gy + 1},
            device_id_type=MESH,
        )

    def send_edges(k):
        pl.when(has_prev)(lambda: y_previous(k).start())
        pl.when(has_next)(lambda: y_next(k).start())

    def take_edges(k):
        @pl.when(has_prev)
        def _():
            y_previous(k).wait_send()
            part = yb.at[k, :, pl.ds(0, SUBLANES)]
            pltpu.make_async_copy(part, part, y_recv.at[k, 0]).wait()

        @pl.when(has_next)
        def _():
            y_next(k).wait_send()
            part = yb.at[k, :, pl.ds(SUBLANES, SUBLANES)]
            pltpu.make_async_copy(part, part, y_recv.at[k, 1]).wait()

    def take_step(k, carry):
        for c in range(nx):
            pltpu.make_async_copy(zf.at[0], recv.at[k, c], recv_sem.at[k, c]).wait()
        send_edges(k)
        x_filter([recv[k, c] for c in range(nx)], w_own, w_edge, xs, 0)
        take_edges(k)
        x_filter([yb[k, c] for c in range(nx)], w_own, w_edge, xs, 2 * rows)

        def put(at, value):
            fstage[k, :, at] = value
            pstage[k, :, at] = projection(value)

        y_filter(xs, scale, scale_along_z(sizes, k, layers, columns), columns, put)
        return carry

    lax.fori_loop(0, final, take_step, 0)

    for c in range(nx):
        for side in range(2):
            part = lrecv.at[c, edges[side]]
            pltpu.make_async_copy(part, part, e_recv.at[side, c]).wait()
    pl.when(has_prev)(lambda: last_previous().start())
    pl.when(has_next)(lambda: last_next().start())

    @pl.when(has_down)
    def _():
        for j in range(RADIUS):
            to_next(j).wait_send()

    @pl.when(has_up)
    def _():
        for j in range(RADIUS):
            to_previous(j).wait_send()

    def settle(k, carry):
        for p in range(nx):

            @pl.when(gx != p)
            def _():
                piece(k, p, 0).wait_send()

        return carry

    lax.fori_loop(0, final, settle, 0)
    for p in range(nx):

        @pl.when(gx != p)
        def _():
            edge_piece(0, p, 0).wait_send()
            edge_piece(1, p, 0).wait_send()
            inner_piece(p, 0).wait_send()

    @pl.when(has_prev)
    def _():
        last_previous().wait_send()
        part = lyb.at[:, pl.ds(0, SUBLANES)]
        pltpu.make_async_copy(part, part, y_recv.at[final, 0]).wait()

    @pl.when(has_next)
    def _():
        last_next().wait_send()
        part = lyb.at[:, pl.ds(SUBLANES, SUBLANES)]
        pltpu.make_async_copy(part, part, y_recv.at[final, 1]).wait()

    for c in range(nx):
        part = lrecv.at[c, inside]
        pltpu.make_async_copy(part, part, recv_sem.at[final, c]).wait()


def closing(sizes, fstage, pstage, lrecv, lyb, scale, w_own, w_edge, filt, proj, xs, flast, plast, sems, last_sems):
    final = fstage.shape[0]
    nx, rows, columns = lrecv.shape
    layers = final + 1

    def finished(k):
        at = layer_of(k, layers)
        return (
            pltpu.make_async_copy(fstage.at[k], filt.at[at], sems.at[0, k]),
            pltpu.make_async_copy(pstage.at[k], proj.at[at], sems.at[1, k]),
        )

    for k in range(final):
        for copy in finished(k):
            copy.start()
    x_filter([lrecv[c] for c in range(nx)], w_own, w_edge, xs, 0)
    x_filter([lyb[c] for c in range(nx)], w_own, w_edge, xs, 2 * rows)

    def put(at, value):
        flast[:, at] = value
        plast[:, at] = projection(value)

    y_filter(xs, scale, scale_along_z(sizes, final, layers, columns), columns, put)
    at = layer_of(final, layers)
    ends = (
        pltpu.make_async_copy(flast, filt.at[at], last_sems.at[0]),
        pltpu.make_async_copy(plast, proj.at[at], last_sems.at[1]),
    )
    for copy in ends:
        copy.start()
    for k in range(final):
        for copy in finished(k):
            copy.wait()
    for copy in ends:
        copy.wait()


def body(sizes, density, mask):
    planes, rows, columns = density.shape
    nz, nx, ny = sizes
    layers = planes // nx
    final = layers - 1
    blocks = mask.shape[0]
    width = nx * columns
    dma = pltpu.SemaphoreType.DMA
    f32, bf16 = jnp.float32, jnp.bfloat16
    shape = jax.ShapeDtypeStruct
    carried = (
        shape((final, rows, width), f32),
        shape((final, rows, width), f32),
        shape((nx, rows, columns), f32),
        shape((nx, 2 * SUBLANES, columns), f32),
        shape((rows, width), f32),
        shape((columns, columns), bf16),
        shape((2 * LANES, columns), bf16),
    )
    xs = pltpu.VMEM((2 * rows + 4 * SUBLANES, width), bf16)
    held = pl.pallas_call(
        functools.partial(kernel, sizes),
        out_shape=carried,
        in_specs=[pl.BlockSpec(memory_space=pl.ANY)] * 2,
        out_specs=(pl.BlockSpec(memory_space=pltpu.VMEM),) * len(carried),
        scratch_shapes=[
            pltpu.VMEM((planes + 2 * RADIUS, rows, columns), f32),
            pltpu.VMEM((blocks + 2, rows, columns), f32),
            pltpu.VMEM((blocks + 2,) + mask.shape[1:], jnp.int32),
            pltpu.VMEM((planes, rows, columns), f32),
            pltpu.VMEM((final, nx, rows, columns), f32),
            pltpu.VMEM((final, nx, 2 * SUBLANES, columns), f32),
            xs,
            dma((blocks,)),
            dma,
            dma((2,)),
            dma((2,)),
            dma((2, RADIUS)),
            dma((2, RADIUS)),
            dma((layers, nx)),
            dma((layers, nx)),
            dma((layers, 2)),
            dma((layers, 2)),
            dma((2, nx)),
            dma((2, nx)),
        ],
        compiler_params=pltpu.CompilerParams(
            collective_id=0, has_side_effects=True, vmem_limit_bytes=44 * 1024 * 1024
        ),
    )(density, mask)
    return pl.pallas_call(
        functools.partial(closing, sizes),
        out_shape=(shape((layers, rows, width), f32),) * 2,
        in_specs=[pl.BlockSpec(memory_space=pltpu.VMEM)] * len(carried),
        out_specs=(pl.BlockSpec(memory_space=pl.ANY),) * 2,
        scratch_shapes=[
            xs,
            pltpu.VMEM((rows, width), f32),
            pltpu.VMEM((rows, width), f32),
            dma((2, final)),
            dma((2,)),
        ],
        compiler_params=pltpu.CompilerParams(vmem_limit_bytes=16 * 1024 * 1024),
    )(*held)


def solution(mesh):
    sizes = (mesh.shape["gz"], mesh.shape["gx"], mesh.shape["gy"])
    placed = (P("gz", "gy", "gx"), P("gz", "gy", "gx"))
    return jax.shard_map(
        functools.partial(body, sizes),
        mesh=mesh,
        in_specs=placed,
        out_specs=(P(("gz", "gx"), "gy", None), P(("gz", "gx"), "gy", None)),
        check_vma=False,
    )
```

profile of v0, /device:TPU:1, one launch (start us, length us, event | category | flops | bytes accessed | tf_op | source)
XLA Modules:
  0.0 58.9 jit_solution(10424264122945561002)
XLA Ops:
  0.6 0.0 copy-start
  0.6 0.7 %copy-done = s32[4,16,32]{2,1,0:T(8,128)S(1)} copy-done((s32[4,16,32]{2,1,0:T(8,128)S(1)}, s32[4,16,32]{2,1,0:T(8,128)}, u32[]{:S(2)}) %copy-start) | copy-done | bytes 8216
  1.4 53.5 %shard_map.41 = (f32[7,128,1024]{2,1,0:T(8,128)S(1)}, f32[7,128,1024]{2,1,0:T(8,128)S(1)}, f32[4,128,256]{2,1,0:T(8,128)S(1)}, f32[4,16,256]{2,1,0:T(8,128)S(1)}...) custom-call(f32[32,128,256]{2,1,0:T(8,128)} %density.1, s32[4,16,32]{2,1,0:T(8,128)S(1)} %copy-done), custom_call_target="tpu_custom_call" | custom-call | tf_op jit(solution)/shard_map/pallas_call | solution.py:588
  54.9 3.9 %shard_map.42 = (f32[8,128,1024]{2,1,0:T(8,128)}, f32[8,128,1024]{2,1,0:T(8,128)}) custom-call(f32[7,128,1024]{2,1,0:T(8,128)S(1)} %get-tuple-element.9.fstage, f32[7,128,1024]{2,1,0:T(8,128)S(1)} %get-tuple-element.10.pstage, f32[4,128,256]{2,1,0:T(8,128)S(1)} %get-tuple-element.11.lrecv, f32[4,16,256]{2,1,0:T(8,128)S(1)} %get-tuple-element.12.lyb, ...), custom_call_target="tpu_custom_call" | custom-call | tf_op jit(solution)/shard_map/pallas_call | solution.py:618
Async XLA Ops:
  0.6 0.8 %copy-start = (s32[4,16,32]{2,1,0:T(8,128)S(1)}, s32[4,16,32]{2,1,0:T(8,128)}, u32[]{:S(2)}) copy-start(s32[4,16,32]{2,1,0:T(8,128)} %mask.1) | copy-start | bytes 24580
where the time goes:
time: 59.6 us; the launch traced here: 58.9 us
  Pallas kernels  57.5 us (96%)
  local copies, waits for them, and re-layouts  0.75 us (1%)
  between operations  0.65 us (1%)
    pallas_call x1, Pallas kernels, body(): pl.pallas_call(functools.partial(kernel, sizes), out_shape=carried, in_sp...  53.5 us
    pallas_call x1, Pallas kernels, body(): pl.pallas_call(functools.partial(closing, sizes), out_shape=(shape((layer...  3.94 us

commit v1 on v0

v1 whole, which is shorter than its diff:
```python
import functools
import math

import jax
import jax.numpy as jnp
from jax import lax
from jax.experimental import pallas as pl
from jax.experimental.pallas import tpu as pltpu
from jax.sharding import PartitionSpec as P

RADIUS = 6
CELLS = 8
LANES = 128
SUBLANES = 8

sharpness = 8.0
threshold = 0.5
MESH = pl.DeviceIdType.MESH


def hat(rows, cols, offset):
    row = lax.broadcasted_iota(jnp.int32, (rows, cols), 0)
    col = lax.broadcasted_iota(jnp.int32, (rows, cols), 1)
    return jnp.maximum(RADIUS + 1 - jnp.abs(col + offset - row), 0).astype(jnp.float32)


def halves(values):
    high = values.astype(jnp.bfloat16)
    low = (values - high.astype(jnp.float32)).astype(jnp.bfloat16)
    return high, low


def projection(filtered):
    top = math.tanh(sharpness * threshold)
    bottom = top + math.tanh(sharpness * (1.0 - threshold))
    return (top + jnp.tanh(sharpness * (filtered - threshold))) * (1.0 / bottom)


def one_side(reach):
    return reach * (RADIUS + 1) - reach * (reach + 1) // 2


def dot(a, b):
    return jnp.dot(a, b, preferred_element_type=jnp.float32)


def x_filter(chunks, w_own, w_edge, xs, first):
    size, columns = chunks[0].shape
    high, low = zip(*[halves(chunk) for chunk in chunks])
    none = jnp.zeros((size, LANES), jnp.bfloat16)
    for c in range(len(chunks)):
        total = dot(high[c], w_own[...]) + dot(low[c], w_own[...])
        for part in (high, low):
            left = part[c - 1][:, columns - LANES :] if c > 0 else none
            right = part[c + 1][:, :LANES] if c < len(chunks) - 1 else none
            total = total + dot(jnp.concatenate([left, right], 1), w_edge[...])
        at = pl.ds(c * columns, columns)
        xs[pl.ds(first, size), at], xs[pl.ds(first + size, size), at] = halves(total)


def y_filter(xs, scale, scale_z, columns, put):
    rows, width = scale.shape
    own = hat(rows, rows, 0).astype(jnp.bfloat16)
    edge = jnp.concatenate([hat(rows, SUBLANES, -SUBLANES), hat(rows, SUBLANES, rows)], 1)
    edge = edge.astype(jnp.bfloat16)
    own = jnp.concatenate([own, own], 1)
    edge = jnp.concatenate([edge, edge], 1)
    for c in range(width // columns):
        at = pl.ds(c * columns, columns)
        summed = dot(own, xs[pl.ds(0, 2 * rows), at])
        summed = summed + dot(edge, xs[pl.ds(2 * rows, 4 * SUBLANES), at])
        put(at, summed * (scale[:, at] * scale_z))


def inverse_count(position, length):
    left = one_side(jnp.minimum(position, RADIUS))
    right = one_side(jnp.minimum(length - 1 - position, RADIUS))
    return 1.0 / (RADIUS + 1 + left + right).astype(jnp.float32)


def layer_of(k, layers):
    return jnp.where(lax.axis_index("gx") == 0, layers - 1 - k, k)


def scale_along_z(sizes, k, layers, columns):
    nz, nx, ny = sizes
    level = (lax.axis_index("gz") * nx + lax.axis_index("gx")) * layers + layer_of(k, layers)
    level = jnp.full((SUBLANES, columns), level, jnp.int32)
    return inverse_count(level, nz * nx * layers)[0:1]


def same(ref):
    return functools.partial(pltpu.make_async_copy, ref, ref)


def wait_sides(first, second, sem, one, both):
    @pl.when(jnp.logical_and(first, second))
    def _():
        same(both)(sem).wait()

    @pl.when(first != second)
    def _():
        same(one)(sem).wait()


def kernel(
    sizes,
    density,
    mask,
    fstage,
    pstage,
    lrecv,
    lyb,
    scale,
    w_own,
    w_edge,
    phys,
    codes,
    masks,
    zf,
    recv,
    yb,
    xs,
    load_sem,
    mask_sem,
    hmask_send,
    hmask_recv,
    halo_send,
    halo_recv,
    send_sem,
    recv_sem,
    y_send,
    y_recv,
    e_recv,
):
    nz, nx, ny = sizes
    planes, rows, columns = density.shape
    blocks, mrows, mcols = mask.shape
    layers = planes // nx
    final = layers - 1
    gz, gx, gy = lax.axis_index("gz"), lax.axis_index("gx"), lax.axis_index("gy")
    has_up, has_down = gz > 0, gz < nz - 1
    has_prev, has_next = gy > 0, gy < ny - 1

    def load(b):
        part = pl.ds(b * CELLS, CELLS)
        return pltpu.make_async_copy(
            density.at[part], phys.at[pl.ds(RADIUS + b * CELLS, CELLS)], load_sem.at[b]
        )

    mask_copy = pltpu.make_async_copy(mask, masks.at[pl.ds(1, blocks)], mask_sem)
    mask_copy.start()
    for b in range(blocks):
        load(b).start()

    barrier = pltpu.get_barrier_semaphore()

    def greet(**where):
        pl.semaphore_signal(barrier, inc=1, device_id=where, device_id_type=MESH)

    for step in range(1, nx):
        greet(gx=lax.rem(gx + step, nx))
    pl.when(has_up)(lambda: greet(gz=gz - 1))
    pl.when(has_down)(lambda: greet(gz=gz + 1))
    pl.when(has_prev)(lambda: greet(gy=gy - 1))
    pl.when(has_next)(lambda: greet(gy=gy + 1))

    def to_next(j):
        return pltpu.make_async_remote_copy(
            src_ref=density.at[planes - 1 - j],
            dst_ref=phys.at[RADIUS - 1 - j],
            send_sem=halo_send,
            recv_sem=halo_recv.at[j],
            device_id={"gz": gz + 1},
            device_id_type=MESH,
        )

    def to_previous(j):
        return pltpu.make_async_remote_copy(
            src_ref=density.at[j],
            dst_ref=phys.at[RADIUS + planes + j],
            send_sem=halo_send,
            recv_sem=halo_recv.at[j],
            device_id={"gz": gz - 1},
            device_id_type=MESH,
        )

    def mask_next():
        return pltpu.make_async_remote_copy(
            src_ref=mask.at[blocks - 1],
            dst_ref=masks.at[0],
            send_sem=hmask_send,
            recv_sem=hmask_recv,
            device_id={"gz": gz + 1},
            device_id_type=MESH,
        )

    def mask_previous():
        return pltpu.make_async_remote_copy(
            src_ref=mask.at[0],
            dst_ref=masks.at[blocks + 1],
            send_sem=hmask_send,
            recv_sem=hmask_recv,
            device_id={"gz": gz - 1},
            device_id_type=MESH,
        )

    def spread(b, count):
        small = masks[pl.ds(b, count)].reshape(count * mrows, mcols)
        small = small.astype(jnp.float32).astype(jnp.bfloat16)
        c = lax.broadcasted_iota(jnp.int32, (mcols, columns), 1) // CELLS
        n = lax.broadcasted_iota(jnp.int32, (mcols, columns), 0)
        wide = jnp.where(c == n, 1.0, 0.0).astype(jnp.bfloat16)
        codes[pl.ds(b * mrows, count * mrows)] = dot(small, wide)

    def apply_mask(row, count, b):
        def one(r, carry):
            at = pl.ds(pl.multiple_of(r * CELLS, CELLS), CELLS)
            code = jnp.broadcast_to(codes[pl.ds(b * mrows + r, 1)], (CELLS, columns))
            void, solid = code < 0.5, code < 1.5
            for i in range(count):
                held = phys[row + i, at]
                phys[row + i, at] = jnp.where(void, 0.0, jnp.where(solid, 1.0, held))
            return carry

        lax.fori_loop(0, mrows, one, 0, unroll=4 if count > 1 else 8)

    def piece(k, p, row):
        return pltpu.make_async_remote_copy(
            src_ref=zf.at[row],
            dst_ref=recv.at[k, gx],
            send_sem=send_sem,
            recv_sem=recv_sem.at[k],
            device_id={"gx": p},
            device_id_type=MESH,
        )

    edges = (pl.ds(0, SUBLANES), pl.ds(rows - SUBLANES, SUBLANES))
    inside = pl.ds(SUBLANES, rows - 2 * SUBLANES)

    def edge_piece(side, p, row):
        return pltpu.make_async_remote_copy(
            src_ref=zf.at[row, edges[side]],
            dst_ref=lrecv.at[gx, edges[side]],
            send_sem=send_sem,
            recv_sem=e_recv,
            device_id={"gx": p},
            device_id_type=MESH,
        )

    def inner_piece(p, row):
        return pltpu.make_async_remote_copy(
            src_ref=zf.at[row, inside],
            dst_ref=lrecv.at[gx, inside],
            send_sem=send_sem,
            recv_sem=recv_sem.at[final],
            device_id={"gx": p},
            device_id_type=MESH,
        )

    def row_of(k, p):
        return final - k if p == 0 else p * layers + k

    def z_filter(row, out):
        part = rows // 4
        for i in range(4):
            at = pl.ds(i * part, part)
            run = phys[row + RADIUS, at]
            total = run
            for d in range(1, RADIUS + 1):
                run = run + (phys[row + RADIUS - d, at] + phys[row + RADIUS + d, at])
                total = total + run
            out[at] = total

    def z_send(k, p):
        row = row_of(k, p)

        @pl.when(gx != p)
        def _():
            z_filter(row, zf.at[row])
            piece(k, p, row).start()

        @pl.when(gx == p)
        def _():
            z_filter(row, recv.at[k, p])

    def z_step(k, carry):
        for p in range(nx):
            z_send(k, p)
        return carry

    mask_copy.wait()
    spread(1, blocks)
    ready = 0
    for p in range(nx):
        need = min(blocks, (row_of(0, p) + RADIUS) // CELLS + 1)
        for b in range(ready, need):
            load(b).wait()
            apply_mask(RADIUS + b * CELLS, CELLS, b + 1)
        if p == 0:
            count = nx - 1
            for there in (has_up, has_down, has_prev, has_next):
                count = count + there.astype(jnp.int32)
            pl.semaphore_wait(barrier, count)
        ready = max(ready, need)
        z_send(0, p)
    for b in range(ready, blocks):
        load(b).wait()
        apply_mask(RADIUS + b * CELLS, CELLS, b + 1)

    @pl.when(has_down)
    def _():
        mask_next().start()
        for j in range(RADIUS):
            to_next(j).start()

    @pl.when(has_up)
    def _():
        mask_previous().start()
        for j in range(RADIUS):
            to_previous(j).start()

    free = layers - RADIUS
    lax.fori_loop(1, free, z_step, 0)

    @pl.when(jnp.logical_not(has_up))
    def _():
        phys[pl.ds(0, RADIUS)] = jnp.zeros((RADIUS, rows, columns), jnp.float32)

    @pl.when(jnp.logical_not(has_down))
    def _():
        phys[pl.ds(RADIUS + planes, RADIUS)] = jnp.zeros((RADIUS, rows, columns), jnp.float32)

    @pl.when(jnp.logical_not(has_prev))
    def _():
        lyb[:, pl.ds(0, SUBLANES)] = jnp.zeros((nx, SUBLANES, columns), jnp.float32)
        yb[:, :, pl.ds(0, SUBLANES)] = jnp.zeros((final, nx, SUBLANES, columns), jnp.float32)

    @pl.when(jnp.logical_not(has_next))
    def _():
        lyb[:, pl.ds(SUBLANES, SUBLANES)] = jnp.zeros((nx, SUBLANES, columns), jnp.float32)
        yb[:, :, pl.ds(SUBLANES, SUBLANES)] = jnp.zeros((final, nx, SUBLANES, columns), jnp.float32)

    w_own[...] = hat(columns, columns, 0).astype(jnp.bfloat16)
    w_edge[pl.ds(0, LANES)] = hat(LANES, columns, LANES).astype(jnp.bfloat16)
    w_edge[pl.ds(LANES, LANES)] = hat(LANES, columns, -columns).astype(jnp.bfloat16)

    width = nx * columns
    scale_y = inverse_count(
        gy * rows + lax.broadcasted_iota(jnp.int32, (rows, LANES), 0), rows * ny
    )
    for c in range(0, width, LANES):
        lane = c + lax.broadcasted_iota(jnp.int32, (SUBLANES, LANES), 1)
        scale_x = inverse_count(lane, width)
        scale[:, pl.ds(c, LANES)] = scale_y * scale_x[0:1]

    two = pl.ds(0, 2)
    wait_sides(has_up, has_down, hmask_send, masks.at[0], masks.at[two])
    wait_sides(has_up, has_down, hmask_recv, masks.at[0], masks.at[two])
    pl.when(has_up)(lambda: spread(0, 1))
    pl.when(has_down)(lambda: spread(blocks + 1, 1))

    def take_halo(k):
        j = k - free
        wait_sides(has_up, has_down, halo_recv.at[j], zf.at[0], zf.at[two])
        pl.when(has_up)(lambda: apply_mask(RADIUS - 1 - j, 1, 0))
        pl.when(has_down)(lambda: apply_mask(RADIUS + planes + j, 1, blocks + 1))

    def halo_step(k, carry):
        take_halo(k)
        return z_step(k, carry)

    lax.fori_loop(free, final, halo_step, 0)

    take_halo(final)
    for p in range(nx):
        row = row_of(final, p)

        @pl.when(gx != p)
        def _():
            z_filter(row, zf.at[row])
            edge_piece(0, p, row).start()
            edge_piece(1, p, row).start()

        @pl.when(gx == p)
        def _():
            z_filter(row, lrecv.at[p])

    for p in range(nx):

        @pl.when(gx != p)
        def _():
            inner_piece(p, row_of(final, p)).start()

    top, bottom = pl.ds(0, SUBLANES), pl.ds(SUBLANES, SUBLANES)

    def edge_to(where, k, held, side, landing, into):
        return pltpu.make_async_remote_copy(
            src_ref=held.at[:, edges[side]],
            dst_ref=landing.at[:, into],
            send_sem=y_send,
            recv_sem=y_recv.at[k],
            device_id={"gy": where},
            device_id_type=MESH,
        )

    def send_edges(k, held, landing):
        pl.when(has_prev)(lambda: edge_to(gy - 1, k, held, 0, landing, bottom).start())
        pl.when(has_next)(lambda: edge_to(gy + 1, k, held, 1, landing, top).start())

    def take_edges(k):
        wait_sides(has_prev, has_next, y_recv.at[k], lyb.at[:, top], lyb)

    def arrive(k):
        same(zf.at[pl.ds(0, nx - 1)])(recv_sem.at[k]).wait()
        send_edges(k, recv.at[k], yb.at[k])

    def process(k):
        x_filter([recv[k, c] for c in range(nx)], w_own, w_edge, xs, 0)
        take_edges(k)
        x_filter([yb[k, c] for c in range(nx)], w_own, w_edge, xs, 2 * rows)

        def put(at, value):
            fstage[k, :, at] = value
            pstage[k, :, at] = projection(value)

        y_filter(xs, scale, scale_along_z(sizes, k, layers, columns), columns, put)

    def take_step(k, carry):
        arrive(k)
        process(k - 1)
        return carry

    arrive(0)
    lax.fori_loop(1, final, take_step, 0)

    same(lrecv.at[pl.ds(0, nx - 1), pl.ds(0, 2 * SUBLANES)])(e_recv).wait()
    send_edges(final, lrecv, lyb)
    process(final - 1)

    half, whole = pl.ds(0, RADIUS), pl.ds(0, 2 * RADIUS)
    wait_sides(has_up, has_down, halo_send, zf.at[half], zf.at[whole])
    per_plane = columns * rows // (nx * SUBLANES * columns)
    half, whole = pl.ds(0, layers // per_plane), pl.ds(0, 2 * layers // per_plane)
    wait_sides(has_prev, has_next, y_send, zf.at[half], zf.at[whole])
    same(zf.at[pl.ds(0, (nx - 1) * layers)])(send_sem).wait()
    take_edges(final)
    same(lrecv.at[pl.ds(0, nx - 1), inside])(recv_sem.at[final]).wait()


def closing(sizes, fstage, pstage, lrecv, lyb, scale, w_own, w_edge, filt, proj, xs, flast, plast, sems):
    final = fstage.shape[0]
    nx, rows, columns = lrecv.shape
    layers = final + 1

    def finished(k, carry):
        at = layer_of(k, layers)
        pltpu.make_async_copy(fstage.at[k], filt.at[at], sems.at[0]).start()
        pltpu.make_async_copy(pstage.at[k], proj.at[at], sems.at[1]).start()
        return carry

    lax.fori_loop(0, final, finished, 0)
    x_filter([lrecv[c] for c in range(nx)], w_own, w_edge, xs, 0)
    x_filter([lyb[c] for c in range(nx)], w_own, w_edge, xs, 2 * rows)

    def put(at, value):
        flast[:, at] = value
        plast[:, at] = projection(value)

    y_filter(xs, scale, scale_along_z(sizes, final, layers, columns), columns, put)
    at = layer_of(final, layers)
    pltpu.make_async_copy(flast, filt.at[at], sems.at[0]).start()
    pltpu.make_async_copy(plast, proj.at[at], sems.at[1]).start()
    same(filt)(sems.at[0]).wait()
    same(proj)(sems.at[1]).wait()


def body(sizes, density, mask):
    planes, rows, columns = density.shape
    nz, nx, ny = sizes
    layers = planes // nx
    final = layers - 1
    blocks = mask.shape[0]
    width = nx * columns
    dma = pltpu.SemaphoreType.DMA
    f32, bf16 = jnp.float32, jnp.bfloat16
    shape = jax.ShapeDtypeStruct
    carried = (
        shape((final, rows, width), f32),
        shape((final, rows, width), f32),
        shape((nx, rows, columns), f32),
        shape((nx, 2 * SUBLANES, columns), f32),
        shape((rows, width), f32),
        shape((columns, columns), bf16),
        shape((2 * LANES, columns), bf16),
    )
    xs = pltpu.VMEM((2 * rows + 4 * SUBLANES, width), bf16)
    held = pl.pallas_call(
        functools.partial(kernel, sizes),
        out_shape=carried,
        in_specs=[pl.BlockSpec(memory_space=pltpu.HBM)] * 2,
        out_specs=(pl.BlockSpec(memory_space=pltpu.VMEM),) * len(carried),
        scratch_shapes=[
            pltpu.VMEM((planes + 2 * RADIUS, rows, columns), f32),
            pltpu.VMEM(((blocks + 2) * mask.shape[1], columns), f32),
            pltpu.VMEM((blocks + 2,) + mask.shape[1:], jnp.int32),
            pltpu.VMEM((planes, rows, columns), f32),
            pltpu.VMEM((final, nx, rows, columns), f32),
            pltpu.VMEM((final, nx, 2 * SUBLANES, columns), f32),
            xs,
            dma((blocks,)),
            dma,
            dma,
            dma,
            dma,
            dma((RADIUS,)),
            dma,
            dma((layers,)),
            dma,
            dma((layers,)),
            dma,
        ],
        compiler_params=pltpu.CompilerParams(
            collective_id=0, has_side_effects=True, vmem_limit_bytes=44 * 1024 * 1024
        ),
    )(density, pltpu.with_memory_space_constraint(mask, pltpu.HBM))
    return pl.pallas_call(
        functools.partial(closing, sizes),
        out_shape=(shape((layers, rows, width), f32),) * 2,
        in_specs=[pl.BlockSpec(memory_space=pltpu.VMEM)] * len(carried),
        out_specs=(pl.BlockSpec(memory_space=pl.ANY),) * 2,
        scratch_shapes=[
            xs,
            pltpu.VMEM((rows, width), f32),
            pltpu.VMEM((rows, width), f32),
            dma((2,)),
        ],
        compiler_params=pltpu.CompilerParams(vmem_limit_bytes=16 * 1024 * 1024),
    )(*held)


def solution(mesh):
    sizes = (mesh.shape["gz"], mesh.shape["gx"], mesh.shape["gy"])
    placed = (P("gz", "gy", "gx"), P("gz", "gy", "gx"))
    return jax.shard_map(
        functools.partial(body, sizes),
        mesh=mesh,
        in_specs=placed,
        out_specs=(P(("gz", "gx"), "gy", None), P(("gz", "gx"), "gy", None)),
        check_vma=False,
    )
```

time: 59.6 us -> 56.1 us (0.941)
  Pallas kernels: 57.5 us -> 55 us
  local copies, waits for them, and re-layouts: 0.75 us -> 0 us
    pallas_call x1, Pallas kernels: 53.5 us -> 51.7 us  [body(): pl.pallas_call(functools.partial(kernel, sizes), out_shape=carried, in_sp...]
    unnamed x2 -> x0, local copies, waits for them, and re-layouts: 0.75 us -> none
    pallas_call x1, Pallas kernels: 3.94 us -> 3.3 us  [body(): pl.pallas_call(functools.partial(closing, sizes), out_shape=(shape((layer...]
where the time goes in v1:
time: 56.1 us; the launch traced here: 55.7 us
  Pallas kernels  55 us (98%)
  between operations  0.64 us (1%)
    pallas_call x1, Pallas kernels, body(): pl.pallas_call(functools.partial(kernel, sizes), out_shape=carried, in_sp...  51.7 us
    pallas_call x1, Pallas kernels, body(): pl.pallas_call(functools.partial(closing, sizes), out_shape=(shape((layer...  3.3 us

profile of v1, /device:TPU:1, one launch (start us, length us, event | category | flops | bytes accessed | tf_op | source)
XLA Modules:
  0.0 55.7 jit_solution(3891273095037417223)
XLA Ops:
  0.6 51.7 %shard_map.41 = (f32[7,128,1024]{2,1,0:T(8,128)S(1)}, f32[7,128,1024]{2,1,0:T(8,128)S(1)}, f32[4,128,256]{2,1,0:T(8,128)S(1)}, f32[4,16,256]{2,1,0:T(8,128)S(1)}...) custom-call(f32[32,128,256]{2,1,0:T(8,128)} %density.1, s32[4,16,32]{2,1,0:T(8,128)} %mask.1), custom_call_target="tpu_custom_call" | custom-call | tf_op jit(solution)/shard_map/pallas_call | solution.py:498
  52.4 3.3 %shard_map.42 = (f32[8,128,1024]{2,1,0:T(8,128)}, f32[8,128,1024]{2,1,0:T(8,128)}) custom-call(f32[7,128,1024]{2,1,0:T(8,128)S(1)} %get-tuple-element.9.fstage, f32[7,128,1024]{2,1,0:T(8,128)S(1)} %get-tuple-element.10.pstage, f32[4,128,256]{2,1,0:T(8,128)S(1)} %get-tuple-element.11.lrecv, f32[4,16,256]{2,1,0:T(8,128)S(1)} %get-tuple-element.12.lyb, ...), custom_call_target="tpu_custom_call" | custom-call | tf_op jit(solution)/shard_map/pallas_call | solution.py:527

commit v2 on v1

--- a/solution.py
+++ b/solution.py
@@ -132,6 +132,9 @@
     y_send,
     y_recv,
     e_recv,
+    ready_x,
+    ready_y,
+    ready_z,
 ):
     nz, nx, ny = sizes
     planes, rows, columns = density.shape
@@ -141,6 +144,16 @@
     gz, gx, gy = lax.axis_index("gz"), lax.axis_index("gx"), lax.axis_index("gy")
     has_up, has_down = gz > 0, gz < nz - 1
     has_prev, has_next = gy > 0, gy < ny - 1
+    odd = lax.rem(gy, 2) == 1
+    sides = has_prev.astype(jnp.int32) + has_next.astype(jnp.int32)
+
+    barrier = pltpu.get_barrier_semaphore()
+
+    def greet(sem, **where):
+        pl.semaphore_signal(sem, inc=1, device_id=where, device_id_type=MESH)
+
+    later = tuple(lax.rem(gx + p, nx) for p in (3, 2, 1))
+    order = tuple(p + (gx <= p).astype(jnp.int32) for p in range(nx - 1))
 
     def load(b):
         part = pl.ds(b * CELLS, CELLS)
@@ -150,20 +163,15 @@
 
     mask_copy = pltpu.make_async_copy(mask, masks.at[pl.ds(1, blocks)], mask_sem)
     mask_copy.start()
-    for b in range(blocks):
+    load(0).start()
+    load(1).start()
+    for p in range(1, nx):
+        pl.when(gx < p)(lambda: greet(barrier, gx=p))
+    pl.when(has_down)(lambda: greet(barrier, gz=gz + 1))
+    pl.when(odd & has_next)(lambda: greet(barrier, gy=gy + 1))
+    pl.when(odd)(lambda: greet(barrier, gy=gy - 1))
+    for b in range(2, blocks):
         load(b).start()
-
-    barrier = pltpu.get_barrier_semaphore()
-
-    def greet(**where):
-        pl.semaphore_signal(barrier, inc=1, device_id=where, device_id_type=MESH)
-
-    for step in range(1, nx):
-        greet(gx=lax.rem(gx + step, nx))
-    pl.when(has_up)(lambda: greet(gz=gz - 1))
-    pl.when(has_down)(lambda: greet(gz=gz + 1))
-    pl.when(has_prev)(lambda: greet(gy=gy - 1))
-    pl.when(has_next)(lambda: greet(gy=gy + 1))
 
     def to_next(j):
         return pltpu.make_async_remote_copy(
@@ -238,28 +246,18 @@
     edges = (pl.ds(0, SUBLANES), pl.ds(rows - SUBLANES, SUBLANES))
     inside = pl.ds(SUBLANES, rows - 2 * SUBLANES)
 
-    def edge_piece(side, p, row):
-        return pltpu.make_async_remote_copy(
-            src_ref=zf.at[row, edges[side]],
-            dst_ref=lrecv.at[gx, edges[side]],
+    def part_piece(k, p, landing, part, sem):
+        return pltpu.make_async_remote_copy(
+            src_ref=zf.at[row_of(k, p), part],
+            dst_ref=landing.at[gx, part],
             send_sem=send_sem,
-            recv_sem=e_recv,
+            recv_sem=sem,
             device_id={"gx": p},
             device_id_type=MESH,
         )
 
-    def inner_piece(p, row):
-        return pltpu.make_async_remote_copy(
-            src_ref=zf.at[row, inside],
-            dst_ref=lrecv.at[gx, inside],
-            send_sem=send_sem,
-            recv_sem=recv_sem.at[final],
-            device_id={"gx": p},
-            device_id_type=MESH,
-        )
-
     def row_of(k, p):
-        return final - k if p == 0 else p * layers + k
+        return jnp.where(p == 0, final - k, p * layers + k)
 
     def z_filter(row, out):
         part = rows // 4
@@ -274,51 +272,65 @@
 
     def z_send(k, p):
         row = row_of(k, p)
-
-        @pl.when(gx != p)
+        z_filter(row, zf.at[row])
+        piece(k, p, row).start()
+
+    def z_step(k, carry):
+        for p in later:
+            z_send(k, p)
+        z_filter(row_of(k, gx), recv.at[k, gx])
+        return carry
+
+    def take_block(b):
+        load(b).wait()
+        apply_mask(RADIUS + b * CELLS, CELLS, b + 1)
+
+    def ready(p):
+        @pl.when(p > gx)
         def _():
-            z_filter(row, zf.at[row])
-            piece(k, p, row).start()
-
-        @pl.when(gx == p)
-        def _():
-            z_filter(row, recv.at[k, p])
-
-    def z_step(k, carry):
-        for p in range(nx):
-            z_send(k, p)
-        return carry
-
+            pl.semaphore_wait(ready_x.at[p], 1)
+
+    earlier = gx + has_up.astype(jnp.int32) + jnp.where(odd, 0, sides)
+    pl.when(earlier > 0)(lambda: pl.semaphore_wait(barrier, earlier))
+    for p in range(nx - 1):
+        pl.when(p < gx)(lambda: greet(ready_x.at[gx], gx=p))
+    pl.when(has_up)(lambda: greet(ready_z, gz=gz - 1))
+    pl.when(jnp.logical_not(odd) & has_prev)(lambda: greet(ready_y, gy=gy - 1))
+    pl.when(jnp.logical_not(odd))(lambda: greet(ready_y, gy=gy + 1))
     mask_copy.wait()
     spread(1, blocks)
-    ready = 0
-    for p in range(nx):
-        need = min(blocks, (row_of(0, p) + RADIUS) // CELLS + 1)
-        for b in range(ready, need):
-            load(b).wait()
-            apply_mask(RADIUS + b * CELLS, CELLS, b + 1)
-        if p == 0:
-            count = nx - 1
-            for there in (has_up, has_down, has_prev, has_next):
-                count = count + there.astype(jnp.int32)
-            pl.semaphore_wait(barrier, count)
-        ready = max(ready, need)
+    take_block(0)
+    take_block(1)
+    ready(order[0])
+    z_send(0, order[0])
+    pl.when(gx > 1)(lambda: z_send(0, order[1]))
+    for b in range(2, blocks):
+        take_block(b)
+
+    @pl.when(gx <= 1)
+    def _():
+        ready(order[1])
+        z_send(0, order[1])
+
+    for p in order[2:]:
+        ready(p)
         z_send(0, p)
-    for b in range(ready, blocks):
-        load(b).wait()
-        apply_mask(RADIUS + b * CELLS, CELLS, b + 1)
+    z_filter(row_of(0, gx), recv.at[0, gx])
+
+    @pl.when(has_up)
+    def _():
+        mask_previous().start()
+        for j in range(RADIUS):
+            to_previous(j).start()
 
     @pl.when(has_down)
     def _():
+        pl.semaphore_wait(ready_z, 1)
         mask_next().start()
         for j in range(RADIUS):
             to_next(j).start()
 
-    @pl.when(has_up)
-    def _():
-        mask_previous().start()
-        for j in range(RADIUS):
-            to_previous(j).start()
+    pl.when(odd)(lambda: pl.semaphore_wait(ready_y, sides))
 
     free = layers - RADIUS
     lax.fori_loop(1, free, z_step, 0)
@@ -370,27 +382,22 @@
         take_halo(k)
         return z_step(k, carry)
 
-    lax.fori_loop(free, final, halo_step, 0)
-
-    take_halo(final)
-    for p in range(nx):
-        row = row_of(final, p)
-
-        @pl.when(gx != p)
-        def _():
-            z_filter(row, zf.at[row])
-            edge_piece(0, p, row).start()
-            edge_piece(1, p, row).start()
-
-        @pl.when(gx == p)
-        def _():
-            z_filter(row, lrecv.at[p])
-
-    for p in range(nx):
-
-        @pl.when(gx != p)
-        def _():
-            inner_piece(p, row_of(final, p)).start()
+    before = final - 1
+    lax.fori_loop(free, before, halo_step, 0)
+
+    last = ((before, recv.at[before]), (final, lrecv))
+    for k, landing in last:
+        take_halo(k)
+        for p in later:
+            z_filter(row_of(k, p), zf.at[row_of(k, p)])
+        z_filter(row_of(k, gx), landing.at[gx])
+    for k, landing in last:
+        for p in later:
+            for side in edges:
+                part_piece(k, p, landing, side, e_recv).start()
+    for k, landing in last:
+        for p in later:
+            part_piece(k, p, landing, inside, recv_sem.at[k]).start()
 
     top, bottom = pl.ds(0, SUBLANES), pl.ds(SUBLANES, SUBLANES)
 
@@ -431,12 +438,18 @@
         process(k - 1)
         return carry
 
+    def inner(k):
+        same(lrecv.at[pl.ds(0, nx - 1), inside])(recv_sem.at[k]).wait()
+
     arrive(0)
-    lax.fori_loop(1, final, take_step, 0)
-
-    same(lrecv.at[pl.ds(0, nx - 1), pl.ds(0, 2 * SUBLANES)])(e_recv).wait()
+    lax.fori_loop(1, before, take_step, 0)
+
+    same(lrecv.at[pl.ds(0, nx - 1), pl.ds(0, 4 * SUBLANES)])(e_recv).wait()
+    send_edges(before, recv.at[before], yb.at[before])
     send_edges(final, lrecv, lyb)
-    process(final - 1)
+    process(before - 1)
+    inner(before)
+    process(before)
 
     half, whole = pl.ds(0, RADIUS), pl.ds(0, 2 * RADIUS)
     wait_sides(has_up, has_down, halo_send, zf.at[half], zf.at[whole])
@@ -445,7 +458,7 @@
     wait_sides(has_prev, has_next, y_send, zf.at[half], zf.at[whole])
     same(zf.at[pl.ds(0, (nx - 1) * layers)])(send_sem).wait()
     take_edges(final)
-    same(lrecv.at[pl.ds(0, nx - 1), inside])(recv_sem.at[final]).wait()
+    inner(final)
 
 
 def closing(sizes, fstage, pstage, lrecv, lyb, scale, w_own, w_edge, filt, proj, xs, flast, plast, sems):
@@ -519,6 +532,9 @@
             dma,
             dma((layers,)),
             dma,
+            pltpu.SemaphoreType.REGULAR((nx,)),
+            pltpu.SemaphoreType.REGULAR,
+            pltpu.SemaphoreType.REGULAR,
         ],
         compiler_params=pltpu.CompilerParams(
             collective_id=0, has_side_effects=True, vmem_limit_bytes=44 * 1024 * 1024

time: 56.1 us -> 55.2 us (0.984)
  Pallas kernels: 55 us -> 54.4 us
    pallas_call x1, Pallas kernels: 51.7 us -> 51.1 us  [body(): pl.pallas_call(functools.partial(kernel, sizes), out_shape=carried, in_sp...]
where the time goes in v2:
time: 55.2 us; the launch traced here: 55.1 us
  Pallas kernels  54.4 us (99%)
  between operations  0.64 us (1%)
    pallas_call x1, Pallas kernels, body(): pl.pallas_call(functools.partial(kernel, sizes), out_shape=carried, in_sp...  51.1 us
    pallas_call x1, Pallas kernels, body(): pl.pallas_call(functools.partial(closing, sizes), out_shape=(shape((layer...  3.3 us

profile of v2, /device:TPU:1, one launch (start us, length us, event | category | flops | bytes accessed | tf_op | source)
XLA Modules:
  0.0 55.1 jit_solution(7422582344023140921)
XLA Ops:
  0.6 51.1 %shard_map.41 = (f32[7,128,1024]{2,1,0:T(8,128)S(1)}, f32[7,128,1024]{2,1,0:T(8,128)S(1)}, f32[4,128,256]{2,1,0:T(8,128)S(1)}, f32[4,16,256]{2,1,0:T(8,128)S(1)}...) custom-call(f32[32,128,256]{2,1,0:T(8,128)} %density.1, s32[4,16,32]{2,1,0:T(8,128)} %mask.1), custom_call_target="tpu_custom_call" | custom-call | tf_op jit(solution)/shard_map/pallas_call | solution.py:511
  51.8 3.3 %shard_map.42 = (f32[8,128,1024]{2,1,0:T(8,128)}, f32[8,128,1024]{2,1,0:T(8,128)}) custom-call(f32[7,128,1024]{2,1,0:T(8,128)S(1)} %get-tuple-element.9.fstage, f32[7,128,1024]{2,1,0:T(8,128)S(1)} %get-tuple-element.10.pstage, f32[4,128,256]{2,1,0:T(8,128)S(1)} %get-tuple-element.11.lrecv, f32[4,16,256]{2,1,0:T(8,128)S(1)} %get-tuple-element.12.lyb, ...), custom_call_target="tpu_custom_call" | custom-call | tf_op jit(solution)/shard_map/pallas_call | solution.py:543

commit v3 on v2

--- a/solution.py
+++ b/solution.py
@@ -122,6 +122,7 @@
     yb,
     xs,
     load_sem,
+    part_sem,
     mask_sem,
     hmask_send,
     hmask_recv,
@@ -132,7 +133,6 @@
     y_send,
     y_recv,
     e_recv,
-    ready_x,
     ready_y,
     ready_z,
 ):
@@ -153,24 +153,37 @@
         pl.semaphore_signal(sem, inc=1, device_id=where, device_id_type=MESH)
 
     later = tuple(lax.rem(gx + p, nx) for p in (3, 2, 1))
-    order = tuple(p + (gx <= p).astype(jnp.int32) for p in range(nx - 1))
+    ahead = 2
+    parts = 4
+    part_rows = rows // parts
+
+    def rows_of(q):
+        return pl.ds(pl.multiple_of(q * part_rows, part_rows), part_rows)
+
+    def load_part(q):
+        return pltpu.make_async_copy(
+            density.at[pl.ds(0, ahead * CELLS), rows_of(q)],
+            phys.at[pl.ds(RADIUS, ahead * CELLS), rows_of(q)],
+            part_sem.at[q],
+        )
 
     def load(b):
         part = pl.ds(b * CELLS, CELLS)
         return pltpu.make_async_copy(
-            density.at[part], phys.at[pl.ds(RADIUS + b * CELLS, CELLS)], load_sem.at[b]
-        )
-
+            density.at[part], phys.at[pl.ds(RADIUS + b * CELLS, CELLS)], load_sem.at[b - ahead]
+        )
+
+    for step in (2, 1, 3):
+        greet(barrier, gx=lax.rem(gx + step, nx))
     mask_copy = pltpu.make_async_copy(mask, masks.at[pl.ds(1, blocks)], mask_sem)
     mask_copy.start()
-    load(0).start()
-    load(1).start()
-    for p in range(1, nx):
-        pl.when(gx < p)(lambda: greet(barrier, gx=p))
+    load_part(0).start()
     pl.when(has_down)(lambda: greet(barrier, gz=gz + 1))
     pl.when(odd & has_next)(lambda: greet(barrier, gy=gy + 1))
     pl.when(odd)(lambda: greet(barrier, gy=gy - 1))
-    for b in range(2, blocks):
+    for q in range(1, parts):
+        load_part(q).start()
+    for b in range(ahead, blocks):
         load(b).start()
 
     def to_next(j):
@@ -221,17 +234,30 @@
         wide = jnp.where(c == n, 1.0, 0.0).astype(jnp.bfloat16)
         codes[pl.ds(b * mrows, count * mrows)] = dot(small, wide)
 
+    def apply_rows(row, count, b, r):
+        at = pl.ds(pl.multiple_of(r * CELLS, CELLS), CELLS)
+        code = jnp.broadcast_to(codes[pl.ds(b * mrows + r, 1)], (CELLS, columns))
+        void, solid = code < 0.5, code < 1.5
+        for i in range(count):
+            held = phys[row + i, at]
+            phys[row + i, at] = jnp.where(void, 0.0, jnp.where(solid, 1.0, held))
+
     def apply_mask(row, count, b):
         def one(r, carry):
-            at = pl.ds(pl.multiple_of(r * CELLS, CELLS), CELLS)
-            code = jnp.broadcast_to(codes[pl.ds(b * mrows + r, 1)], (CELLS, columns))
-            void, solid = code < 0.5, code < 1.5
-            for i in range(count):
-                held = phys[row + i, at]
-                phys[row + i, at] = jnp.where(void, 0.0, jnp.where(solid, 1.0, held))
+            apply_rows(row, count, b, r)
             return carry
 
         lax.fori_loop(0, mrows, one, 0, unroll=4 if count > 1 else 8)
+
+    def first_piece(p, row, at):
+        return pltpu.make_async_remote_copy(
+            src_ref=zf.at[row, at],
+            dst_ref=recv.at[0, gx, at],
+            send_sem=send_sem,
+            recv_sem=recv_sem.at[0],
+            device_id={"gx": p},
+            device_id_type=MESH,
+        )
 
     def piece(k, p, row):
         return pltpu.make_async_remote_copy(
@@ -257,18 +283,21 @@
         )
 
     def row_of(k, p):
+        if isinstance(p, int):
+            return final - k if p == 0 else p * layers + k
         return jnp.where(p == 0, final - k, p * layers + k)
 
+    def z_part(row, at, out):
+        run = phys[row + RADIUS, at]
+        total = run
+        for d in range(1, RADIUS + 1):
+            run = run + (phys[row + RADIUS - d, at] + phys[row + RADIUS + d, at])
+            total = total + run
+        out[at] = total
+
     def z_filter(row, out):
-        part = rows // 4
-        for i in range(4):
-            at = pl.ds(i * part, part)
-            run = phys[row + RADIUS, at]
-            total = run
-            for d in range(1, RADIUS + 1):
-                run = run + (phys[row + RADIUS - d, at] + phys[row + RADIUS + d, at])
-                total = total + run
-            out[at] = total
+        for q in range(parts):
+            z_part(row, pl.ds(q * part_rows, part_rows), out)
 
     def z_send(k, p):
         row = row_of(k, p)
@@ -281,47 +310,48 @@
         z_filter(row_of(k, gx), recv.at[k, gx])
         return carry
 
-    def take_block(b):
+    def first_part(q, carry):
+        at = rows_of(q)
+        load_part(q).wait()
+        for b in range(ahead):
+            for r in range(mrows // parts):
+                apply_rows(RADIUS + b * CELLS, CELLS, b + 1, q * (mrows // parts) + r)
+        for p in range(ahead):
+            row = row_of(0, p)
+
+            @pl.when(gx != p)
+            def _():
+                z_part(row, at, zf.at[row])
+                first_piece(p, row, at).start()
+
+            @pl.when(gx == p)
+            def _():
+                z_part(row, at, recv.at[0, p])
+
+        return carry
+
+    mask_copy.wait()
+    spread(1, blocks)
+    pl.semaphore_wait(barrier, nx - 1 + has_up.astype(jnp.int32) + jnp.where(odd, 0, sides))
+    lax.fori_loop(0, parts, first_part, 0)
+    for b in range(ahead, blocks):
         load(b).wait()
         apply_mask(RADIUS + b * CELLS, CELLS, b + 1)
-
-    def ready(p):
-        @pl.when(p > gx)
-        def _():
-            pl.semaphore_wait(ready_x.at[p], 1)
-
-    earlier = gx + has_up.astype(jnp.int32) + jnp.where(odd, 0, sides)
-    pl.when(earlier > 0)(lambda: pl.semaphore_wait(barrier, earlier))
-    for p in range(nx - 1):
-        pl.when(p < gx)(lambda: greet(ready_x.at[gx], gx=p))
+    for p in range(ahead, nx):
+        pl.when(gx != p)(lambda: z_send(0, p))
+        pl.when(gx == p)(lambda: z_filter(row_of(0, p), recv.at[0, p]))
     pl.when(has_up)(lambda: greet(ready_z, gz=gz - 1))
     pl.when(jnp.logical_not(odd) & has_prev)(lambda: greet(ready_y, gy=gy - 1))
     pl.when(jnp.logical_not(odd))(lambda: greet(ready_y, gy=gy + 1))
-    mask_copy.wait()
-    spread(1, blocks)
-    take_block(0)
-    take_block(1)
-    ready(order[0])
-    z_send(0, order[0])
-    pl.when(gx > 1)(lambda: z_send(0, order[1]))
-    for b in range(2, blocks):
-        take_block(b)
-
-    @pl.when(gx <= 1)
-    def _():
-        ready(order[1])
-        z_send(0, order[1])
-
-    for p in order[2:]:
-        ready(p)
-        z_send(0, p)
-    z_filter(row_of(0, gx), recv.at[0, gx])
 
     @pl.when(has_up)
     def _():
         mask_previous().start()
         for j in range(RADIUS):
             to_previous(j).start()
+
+    free = layers - RADIUS
+    lax.fori_loop(1, free, z_step, 0)
 
     @pl.when(has_down)
     def _():
@@ -331,9 +361,6 @@
             to_next(j).start()
 
     pl.when(odd)(lambda: pl.semaphore_wait(ready_y, sides))
-
-    free = layers - RADIUS
-    lax.fori_loop(1, free, z_step, 0)
 
     @pl.when(jnp.logical_not(has_up))
     def _():
@@ -521,7 +548,8 @@
             pltpu.VMEM((final, nx, rows, columns), f32),
             pltpu.VMEM((final, nx, 2 * SUBLANES, columns), f32),
             xs,
-            dma((blocks,)),
+            dma((blocks - 2,)),
+            dma((4,)),
             dma,
             dma,
             dma,
@@ -532,7 +560,6 @@
             dma,
             dma((layers,)),
             dma,
-            pltpu.SemaphoreType.REGULAR((nx,)),
             pltpu.SemaphoreType.REGULAR,
             pltpu.SemaphoreType.REGULAR,
         ],

time: 55.2 us -> 54.7 us (level)
  no operation moved by 1% of the time
where the time goes in v3:
time: 54.7 us; the launch traced here: 54.6 us
  Pallas kernels  54 us (99%)
  between operations  0.64 us (1%)
    pallas_call x1, Pallas kernels, body(): pl.pallas_call(functools.partial(kernel, sizes), out_shape=carried, in_sp...  50.7 us
    pallas_call x1, Pallas kernels, body(): pl.pallas_call(functools.partial(closing, sizes), out_shape=(shape((layer...  3.3 us

profile of v3, /device:TPU:1, one launch (start us, length us, event | category | flops | bytes accessed | tf_op | source)
XLA Modules:
  0.0 54.6 jit_solution(16066458475483338042)
XLA Ops:
  0.6 50.7 %shard_map.41 = (f32[7,128,1024]{2,1,0:T(8,128)S(1)}, f32[7,128,1024]{2,1,0:T(8,128)S(1)}, f32[4,128,256]{2,1,0:T(8,128)S(1)}, f32[4,16,256]{2,1,0:T(8,128)S(1)}...) custom-call(f32[32,128,256]{2,1,0:T(8,128)} %density.1, s32[4,16,32]{2,1,0:T(8,128)} %mask.1), custom_call_target="tpu_custom_call" | custom-call | tf_op jit(solution)/shard_map/pallas_call | solution.py:538
  51.3 3.3 %shard_map.42 = (f32[8,128,1024]{2,1,0:T(8,128)}, f32[8,128,1024]{2,1,0:T(8,128)}) custom-call(f32[7,128,1024]{2,1,0:T(8,128)S(1)} %get-tuple-element.9.fstage, f32[7,128,1024]{2,1,0:T(8,128)S(1)} %get-tuple-element.10.pstage, f32[4,128,256]{2,1,0:T(8,128)S(1)} %get-tuple-element.11.lrecv, f32[4,16,256]{2,1,0:T(8,128)S(1)} %get-tuple-element.12.lyb, ...), custom_call_target="tpu_custom_call" | custom-call | tf_op jit(solution)/shard_map/pallas_call | solution.py:570

commit v4 on v3

--- a/solution.py
+++ b/solution.py
@@ -133,6 +133,7 @@
     y_send,
     y_recv,
     e_recv,
+    relay,
     ready_y,
     ready_z,
 ):
@@ -152,7 +153,7 @@
     def greet(sem, **where):
         pl.semaphore_signal(sem, inc=1, device_id=where, device_id_type=MESH)
 
-    later = tuple(lax.rem(gx + p, nx) for p in (3, 2, 1))
+    later = tuple(lax.rem(gx + p, nx) for p in (2, 3, 1))
     ahead = 2
     parts = 4
     part_rows = rows // parts
@@ -173,8 +174,9 @@
             density.at[part], phys.at[pl.ds(RADIUS + b * CELLS, CELLS)], load_sem.at[b - ahead]
         )
 
-    for step in (2, 1, 3):
-        greet(barrier, gx=lax.rem(gx + step, nx))
+    right, left = lax.rem(gx + 1, nx), lax.rem(gx + nx - 1, nx)
+    greet(barrier, gx=right)
+    greet(barrier, gx=left)
     mask_copy = pltpu.make_async_copy(mask, masks.at[pl.ds(1, blocks)], mask_sem)
     mask_copy.start()
     load_part(0).start()
@@ -310,36 +312,33 @@
         z_filter(row_of(k, gx), recv.at[k, gx])
         return carry
 
+    parity = lax.rem(gx, 2)
+    near, second, far = 1 - parity, 3 - parity, lax.rem(gx + 2, nx)
+
     def first_part(q, carry):
         at = rows_of(q)
         load_part(q).wait()
         for b in range(ahead):
             for r in range(mrows // parts):
                 apply_rows(RADIUS + b * CELLS, CELLS, b + 1, q * (mrows // parts) + r)
-        for p in range(ahead):
-            row = row_of(0, p)
-
-            @pl.when(gx != p)
-            def _():
-                z_part(row, at, zf.at[row])
-                first_piece(p, row, at).start()
-
-            @pl.when(gx == p)
-            def _():
-                z_part(row, at, recv.at[0, p])
+        row = row_of(0, near)
+        z_part(row, at, zf.at[row])
+        first_piece(near, row, at).start()
 
         return carry
 
     mask_copy.wait()
     spread(1, blocks)
-    pl.semaphore_wait(barrier, nx - 1 + has_up.astype(jnp.int32) + jnp.where(odd, 0, sides))
+    pl.semaphore_wait(barrier, 2 + has_up.astype(jnp.int32) + jnp.where(odd, 0, sides))
+    greet(relay, gx=left)
     lax.fori_loop(0, parts, first_part, 0)
     for b in range(ahead, blocks):
         load(b).wait()
         apply_mask(RADIUS + b * CELLS, CELLS, b + 1)
-    for p in range(ahead, nx):
-        pl.when(gx != p)(lambda: z_send(0, p))
-        pl.when(gx == p)(lambda: z_filter(row_of(0, p), recv.at[0, p]))
+    z_send(0, second)
+    pl.semaphore_wait(relay, 1)
+    z_send(0, far)
+    z_filter(row_of(0, gx), recv.at[0, gx])
     pl.when(has_up)(lambda: greet(ready_z, gz=gz - 1))
     pl.when(jnp.logical_not(odd) & has_prev)(lambda: greet(ready_y, gy=gy - 1))
     pl.when(jnp.logical_not(odd))(lambda: greet(ready_y, gy=gy + 1))
@@ -562,6 +561,7 @@
             dma,
             pltpu.SemaphoreType.REGULAR,
             pltpu.SemaphoreType.REGULAR,
+            pltpu.SemaphoreType.REGULAR,
         ],
         compiler_params=pltpu.CompilerParams(
             collective_id=0, has_side_effects=True, vmem_limit_bytes=44 * 1024 * 1024

time: 54.7 us -> 54.3 us (level); the launches traced: 54.6 us -> 53.6 us
  Pallas kernels: 54 us -> 52.9 us
    pallas_call x1, Pallas kernels: 50.7 us -> 49.6 us  [body(): pl.pallas_call(functools.partial(kernel, sizes), out_shape=carried, in_sp...]
where the time goes in v4:
time: 54.3 us; the launch traced here: 53.6 us
  Pallas kernels  52.9 us (97%)
  between operations  0.64 us (1%)
    pallas_call x1, Pallas kernels, body(): pl.pallas_call(functools.partial(kernel, sizes), out_shape=carried, in_sp...  49.6 us
    pallas_call x1, Pallas kernels, body(): pl.pallas_call(functools.partial(closing, sizes), out_shape=(shape((layer...  3.3 us

profile of v4, /device:TPU:1, one launch (start us, length us, event | category | flops | bytes accessed | tf_op | source)
XLA Modules:
  0.0 53.6 jit_solution(11174389707042865002)
XLA Ops:
  0.6 49.6 %shard_map.41 = (f32[7,128,1024]{2,1,0:T(8,128)S(1)}, f32[7,128,1024]{2,1,0:T(8,128)S(1)}, f32[4,128,256]{2,1,0:T(8,128)S(1)}, f32[4,16,256]{2,1,0:T(8,128)S(1)}...) custom-call(f32[32,128,256]{2,1,0:T(8,128)} %density.1, s32[4,16,32]{2,1,0:T(8,128)} %mask.1), custom_call_target="tpu_custom_call" | custom-call | tf_op jit(solution)/shard_map/pallas_call | solution.py:537
  50.2 3.3 %shard_map.42 = (f32[8,128,1024]{2,1,0:T(8,128)}, f32[8,128,1024]{2,1,0:T(8,128)}) custom-call(f32[7,128,1024]{2,1,0:T(8,128)S(1)} %get-tuple-element.9.fstage, f32[7,128,1024]{2,1,0:T(8,128)S(1)} %get-tuple-element.10.pstage, f32[4,128,256]{2,1,0:T(8,128)S(1)} %get-tuple-element.11.lrecv, f32[4,16,256]{2,1,0:T(8,128)S(1)} %get-tuple-element.12.lyb, ...), custom_call_target="tpu_custom_call" | custom-call | tf_op jit(solution)/shard_map/pallas_call | solution.py:570

commit v5 on v4

--- a/solution.py
+++ b/solution.py
@@ -335,7 +335,7 @@
     for b in range(ahead, blocks):
         load(b).wait()
         apply_mask(RADIUS + b * CELLS, CELLS, b + 1)
-    z_send(0, second)
+        pl.when(second == b)(lambda: z_send(0, second))
     pl.semaphore_wait(relay, 1)
     z_send(0, far)
     z_filter(row_of(0, gx), recv.at[0, gx])

time: 54.3 us -> 54.2 us (level)
  no operation moved by 1% of the time
where the time goes in v5:
time: 54.2 us; the launch traced here: 53.5 us
  Pallas kernels  52.9 us (98%)
  between operations  0.64 us (1%)
    pallas_call x1, Pallas kernels, body(): pl.pallas_call(functools.partial(kernel, sizes), out_shape=carried, in_sp...  49.6 us
    pallas_call x1, Pallas kernels, body(): pl.pallas_call(functools.partial(closing, sizes), out_shape=(shape((layer...  3.3 us

profile of v5, /device:TPU:1, one launch (start us, length us, event | category | flops | bytes accessed | tf_op | source)
XLA Modules:
  0.0 53.5 jit_solution(11150818348969153746)
XLA Ops:
  0.6 49.6 %shard_map.41 = (f32[7,128,1024]{2,1,0:T(8,128)S(1)}, f32[7,128,1024]{2,1,0:T(8,128)S(1)}, f32[4,128,256]{2,1,0:T(8,128)S(1)}, f32[4,16,256]{2,1,0:T(8,128)S(1)}...) custom-call(f32[32,128,256]{2,1,0:T(8,128)} %density.1, s32[4,16,32]{2,1,0:T(8,128)} %mask.1), custom_call_target="tpu_custom_call" | custom-call | tf_op jit(solution)/shard_map/pallas_call | solution.py:537
  50.2 3.3 %shard_map.42 = (f32[8,128,1024]{2,1,0:T(8,128)}, f32[8,128,1024]{2,1,0:T(8,128)}) custom-call(f32[7,128,1024]{2,1,0:T(8,128)S(1)} %get-tuple-element.9.fstage, f32[7,128,1024]{2,1,0:T(8,128)S(1)} %get-tuple-element.10.pstage, f32[4,128,256]{2,1,0:T(8,128)S(1)} %get-tuple-element.11.lrecv, f32[4,16,256]{2,1,0:T(8,128)S(1)} %get-tuple-element.12.lyb, ...), custom_call_target="tpu_custom_call" | custom-call | tf_op jit(solution)/shard_map/pallas_call | solution.py:570
